TPU v7x, 32 devices: a whole 2x2x4 slice. The times are simulated.
32 devices in a mesh: seq: 8 (over z, y), head: 4 (over x, core).
Axes of the slice: x: 2, y: 2, z: 4, core: 2. Of those that a mesh axis runs over, the one named last changes fastest.
Arguments:
- queries: bfloat16 [2048, 4096], P('seq', 'head'), may hold values from -5 to 5
- keys: bfloat16 [2048, 4096], P('seq', 'head'), may hold values from -5 to 5
- values: bfloat16 [2048, 4096], P('seq', 'head'), may hold values from -6 to 6
- beta: float32 [32], P('head'), may hold values from -2 to 2
- w_out: bfloat16 [4096, 4096], P('head'), may hold values from -0.09375 to 0.09375
Outputs:
- mixed: bfloat16 [2048, 4096], P('seq', 'head')
All inputs are finite; a program needn't handle non-finite values.
Results may differ from a plain program's by a relative error of at most 0.0069.
Values may be sent and summed in bfloat16 or wider, within the bound.
A program may use at most 192 MiB of HBM per device.

v0:
```python
import jax
import jax.numpy as jnp
from jax import lax
from jax.sharding import PartitionSpec as P

HD = 128
SEG = 2048


def passed_along(block, axis, distance):
    devices = range(lax.axis_size(axis))
    route = [(i - distance, i) for i in devices if i - distance in devices]
    return lax.ppermute(block, axis, route)


def prefix(part, axis, combine, identity):
    place = lax.axis_index(axis)
    gathered = jax.tree.map(lambda a: lax.all_gather(a, axis), part)
    state = jax.tree.map(lambda a, e: jnp.zeros_like(a) + jnp.asarray(e, a.dtype), part, identity)

    def one(hop, state):
        return combine(
            state, jax.tree.map(lambda a: lax.dynamic_index_in_dim(a, hop, 0, False), gathered)
        )

    return lax.fori_loop(0, place, one, state)


def elu_plus(inputs):
    return jnp.where(inputs > 0, inputs + 1.0, jnp.exp(jnp.minimum(inputs, 0.0)))


def add_pair(earlier, later):
    return (earlier[0] + later[0], earlier[1] + later[1])


def memory_terms(key_block, value_block, heads_here, row_weight):
    token_rows = key_block.shape[0]
    soft_keys = elu_plus(key_block.astype(jnp.float32)).astype(jnp.bfloat16)
    soft_keys = (soft_keys * row_weight[:, None]).reshape(token_rows, heads_here, HD)
    shaped_values = value_block.reshape(token_rows, heads_here, HD)
    outer = jnp.einsum("thd,the->hde", soft_keys, shaped_values, preferred_element_type=jnp.float32)
    totals = jnp.sum(soft_keys, axis=0, dtype=jnp.float32)
    return (outer, totals)


def body(queries, keys, values, beta, w_out):
    token_rows, width = queries.shape
    heads_here = width // HD
    groups = SEG // token_rows
    seq_rank = lax.axis_index("seq")
    place = seq_rank % groups
    stacked = jnp.stack((keys, values))
    earlier_blocks = []
    moving = stacked
    for distance in range(1, groups + 1):
        moving = passed_along(moving, "seq", 1)
        earlier_blocks.append(moving)
    ordered = earlier_blocks[::-1] + [stacked]
    all_keys = jnp.concatenate([block[0] for block in ordered], axis=0)
    all_values = jnp.concatenate([block[1] for block in ordered], axis=0)
    own_ones = jnp.ones((token_rows,), jnp.bfloat16)
    own_outer, own_totals = memory_terms(keys, values, heads_here, own_ones)
    zero_mem = jnp.zeros((heads_here, HD, HD), jnp.float32)
    zero_norm = jnp.zeros((heads_here, HD), jnp.float32)
    memory, norm_prev = prefix((own_outer, own_totals), "seq", add_pair, (zero_mem, zero_norm))
    earlier_rows = groups * token_rows
    row_distance = groups - jnp.arange(earlier_rows) // token_rows
    inside = ((row_distance <= place) & (row_distance < groups)).astype(jnp.bfloat16)
    outer, totals = memory_terms(
        all_keys[:earlier_rows], all_values[:earlier_rows], heads_here, inside
    )
    memory = memory - outer
    norm_prev = norm_prev - totals
    soft_queries = lax.optimization_barrier(
        elu_plus(queries.astype(jnp.float32)).astype(jnp.bfloat16)
    )
    soft_queries = soft_queries.astype(jnp.float32).reshape(token_rows, heads_here, HD)
    numer = jnp.einsum("thd,hde->the", soft_queries, memory, precision=lax.Precision.HIGHEST)
    denom = 1.0 + jnp.einsum("thd,hd->th", soft_queries, norm_prev, precision=lax.Precision.HIGHEST)
    from_memory = numer / denom[..., None]
    scale = HD ** (-0.5)
    key_offset = jnp.arange((groups + 1) * token_rows) - groups * token_rows
    query_offset = jnp.arange(token_rows)
    visible = (
        (key_offset[None, :] <= query_offset[:, None])
        & (key_offset[None, :] > query_offset[:, None] - SEG)
        & (seq_rank * token_rows + key_offset[None, :] >= 0)
    )
    gates = jax.nn.sigmoid(beta)
    outputs = []
    for head_index in range(heads_here):
        lower = head_index * HD
        query_head = queries[:, lower : lower + HD]
        key_head = all_keys[:, lower : lower + HD]
        value_head = all_values[:, lower : lower + HD]
        scores = (
            lax.dot_general(
                query_head, key_head, (((1,), (1,)), ((), ())), preferred_element_type=jnp.float32
            )
            * scale
        )
        scores = jnp.where(visible, scores, -jnp.inf)
        highest = jnp.max(scores, axis=1, keepdims=True)
        weights = jnp.exp(scores - highest)
        total = jnp.sum(weights, axis=1, keepdims=True)
        local = (
            jnp.dot(weights.astype(jnp.bfloat16), value_head, preferred_element_type=jnp.float32)
            / total
        )
        gate = gates[head_index]
        outputs.append(
            (gate * from_memory[:, head_index] + (1.0 - gate) * local).astype(jnp.bfloat16)
        )
    attended = jnp.concatenate(outputs, axis=1)
    partial_out = jnp.dot(attended, w_out, preferred_element_type=jnp.float32)
    summed = lax.psum_scatter(partial_out, "head", scatter_dimension=1, tiled=True)
    return summed.astype(jnp.bfloat16)


def solution(mesh):
    placed = (P("seq", "head"), P("seq", "head"), P("seq", "head"), P("head"), P("head", None))
    return jax.shard_map(
        body, mesh=mesh, in_specs=placed, out_specs=P("seq", "head"), check_vma=False
    )
```

profile of v0, /device:TPU:29, one launch (start us, length us, event | category | flops | bytes accessed | tf_op | source)
XLA Modules:
  0.0 391.7 jit_solution(12818673102016920317)
XLA Ops:
  6.5 2.3 pad_maximum_fusion
  10.2 1.3 convert_reduce_fusion.1
  12.9 27.8 %collective-permute-done = bf16[2,256,1024]{2,1,0:T(8,128)(2,1)S(1)} collective-permute-done((bf16[2,256,1024]{2,1,0:T(8,128)(2,1)}, bf16[2,256,1024]{2,1,0:T(8,128)(2,1)S(1)}, u32[]{:S(2)}, u32[]{:S(2)}) %collective-permute-start) | collective-permute-done | bytes 1048608 | tf_op jit(solution)/shard_map/ppermute | solution.py:13
  42.0 51.4 %collective-permute-done.1 = bf16[2,256,1024]{2,1,0:T(8,128)(2,1)S(1)} collective-permute-done((bf16[2,256,1024]{2,1,0:T(8,128)(2,1)S(1)}, bf16[2,256,1024]{2,1,0:T(8,128)(2,1)S(1)}, u32[]{:S(2)}, u32[]{:S(2)}) %collective-permute-start.1) | collective-permute-done | bytes 1048608 | tf_op jit(solution)/shard_map/ppermute | solution.py:13
  94.7 24.6 %collective-permute-done.2 = bf16[2,256,1024]{2,1,0:T(8,128)(2,1)S(1)} collective-permute-done((bf16[2,256,1024]{2,1,0:T(8,128)(2,1)S(1)}, bf16[2,256,1024]{2,1,0:T(8,128)(2,1)S(1)}, u32[]{:S(2)}, u32[]{:S(2)}) %collective-permute-start.2) | collective-permute-done | bytes 1048608 | tf_op jit(solution)/shard_map/ppermute | solution.py:13
  121.6 37.5 %collective-permute-done.3 = bf16[2,256,1024]{2,1,0:T(8,128)(2,1)S(1)} collective-permute-done((bf16[2,256,1024]{2,1,0:T(8,128)(2,1)S(1)}, bf16[2,256,1024]{2,1,0:T(8,128)(2,1)S(1)}, u32[]{:S(2)}, u32[]{:S(2)}) %collective-permute-start.3) | collective-permute-done | bytes 1048608 | tf_op jit(solution)/shard_map/ppermute | solution.py:13
  162.8 21.8 %collective-permute-done.4 = bf16[2,256,1024]{2,1,0:T(8,128)(2,1)} collective-permute-done((bf16[2,256,1024]{2,1,0:T(8,128)(2,1)S(1)}, bf16[2,256,1024]{2,1,0:T(8,128)(2,1)}, u32[]{:S(2)}, u32[]{:S(2)}) %collective-permute-start.4) | collective-permute-done | bytes 1048608 | tf_op jit(solution)/shard_map/ppermute | solution.py:13
  192.6 34.3 %all_gather.15 = f32[8,8,128]{2,1,0:T(8,128)S(1)} all-gather(f32[1,8,128]{2,1,0:T(8,128)S(1)} %bitcast.245), channel_id=1, replica_groups=mesh['seq'=8,'head'=4] {'seq'}, dimensions={0}, use_global_device_ids=true | all-gather | bytes 36864 | tf_op jit(solution)/shard_map/all_gather | solution.py:18
  241.9 5.8 %collective-permute-done.6 = bf16[2,256,1024]{2,1,0:T(8,128)(2,1)} collective-permute-done((bf16[2,256,1024]{2,1,0:T(8,128)(2,1)}, bf16[2,256,1024]{2,1,0:T(8,128)(2,1)}, u32[]{:S(2)}, u32[]{:S(2)}) %collective-permute-start.6) | collective-permute-done | bytes 1048608 | tf_op jit(solution)/shard_map/ppermute | solution.py:13
  252.2 8.7 %while.12 = (s32[]{:T(128)}, f32[8,128,128]{2,1,0:T(8,128)S(1)}, f32[8,128]{1,0:T(8,128)S(1)}, s32[]{:T(128)}, f32[8,8,128,128]{3,2,1,0:T(8,128)}, /*index=5*/f3...) while((s32[]{:T(128)}, f32[8,128,128]{2,1,0:T(8,128)S(1)}, f32[8,128]{1,0:T(8,128)S(1)}, s32[]{:T(128)}, ...), condition=%wide.region_2.3_spmd, body=%wide.region_1.2_spmd.sunk | while | flops 132101 | bytes 1585295 | solution.py:26
  260.9 8.5 %collective-permute-done.7 = bf16[2,256,1024]{2,1,0:T(8,128)(2,1)} collective-permute-done((bf16[2,256,1024]{2,1,0:T(8,128)(2,1)}, bf16[2,256,1024]{2,1,0:T(8,128)(2,1)}, u32[]{:S(2)}, u32[]{:S(2)}) %collective-permute-start.7) | collective-permute-done | bytes 1048608 | tf_op jit(solution)/shard_map/ppermute | solution.py:13
  269.3 1.4 bitcast_dynamic-update-slice_fusion.23
  270.7 1.5 bitcast_dynamic-update-slice_fusion.21
  272.2 1.5 bitcast_dynamic-update-slice_fusion.19
  273.7 1.4 bitcast_dynamic-update-slice_fusion.17
  283.8 2.2 slice_bitcast_fusion.15
  288.3 7.1 %fusion.7 = bf16[2048,8,128]{2,1,0:T(8,128)(2,1)S(1)} fusion(bf16[2048,8,128]{2,1,0:T(8,128)(2,1)S(1)} %constant_dynamic-update-slice_fusion, bf16[2048]{0:T(1024)(128)(2,1)S(1)} %fusion.243), kind=kLoop, calls=%fused_computation.24 | loop fusion | flops 14680064 | bytes 8392704 | tf_op jit(solution)/shard_map/mul | solution.py:40
  295.4 2.7 convert_reduce_fusion
  304.5 4.7 %fusion.46 = f32[8,128,128]{2,1,0:T(8,128)S(1)} fusion(f32[8,128,128]{2,1,0:T(8,128)S(1)} %get-tuple-element.39, bf16[2048,8,128]{2,1,0:T(8,128)(2,1)} %constant_dynamic-update-slice_fusion.8, bf16[2048,8,128]{2,1,0:T(8,128)(2,1)S(1)} %fusion.7), kind=kOutput, calls=%fused_computation.79 | convolution fusion | flops 537001984 | bytes 9437184 | tf_op jit(solution)/shard_map/thd,the->hde/dot_general | solution.py:42
  316.6 1.3 fusion.174
  319.1 1.4 fusion.162
  322.9 4.5 %fusion.256 = f32[256,4096]{1,0:T(8,128)} fusion(bf16[256,1024]{0,1:T(8,128)(2,1)S(1)} %fusion.150, bf16[1024,4096]{1,0:T(8,128)(2,1)S(1)} %bitcast.220), kind=kOutput, calls=%fused_computation.274 | convolution fusion | flops 2147483648 | bytes 13107200 | tf_op jit(solution)/shard_map/dot_general | solution.py:116
  327.4 55.3 %reduce-scatter.2.cloned.1.call-done = f32[256,1024]{1,0:T(8,128)} async-done(((f32[256,4096]{1,0:T(8,128)}), f32[256,1024]{1,0:T(8,128)}) %reduce-scatter.2.cloned.1.call-update) | async-done | bytes 1048592 | tf_op jit(solution)/shard_map/reduce_scatter | solution.py:117
  382.7 2.1 convert_element_type.118
  (173 shorter events, 69.7 us)
Async XLA Ops:
  6.5 5.2 %copy-start = (bf16[256,1024]{1,0:T(8,128)(2,1)S(1)}, bf16[256,1024]{1,0:T(8,128)(2,1)}, u32[]{:S(2)}) copy-start(bf16[256,1024]{1,0:T(8,128)(2,1)} %param.9) | copy-start | bytes 1572868
  6.5 154.9 %copy-start.25 = (f32[8]{0:T(128)S(1)}, f32[8]{0:T(128)}, u32[]{:S(2)}) copy-start(f32[8]{0:T(128)} %param.10) | copy-start | bytes 100
  6.5 245.6 %all-gather.3.cloned.1.call-start = ((), (), s32[]{:S(2)}) async-start(), calls=%async_computation.2 | async-start | bytes 4718592 | tf_op jit(solution)/shard_map/all_gather | solution.py:18
  8.9 31.9 %collective-permute-start = (bf16[2,256,1024]{2,1,0:T(8,128)(2,1)}, bf16[2,256,1024]{2,1,0:T(8,128)(2,1)S(1)}, u32[]{:S(2)}, u32[]{:S(2)}) collective-permute-start(bf16[2,256,1024]{2,1,0:T(8,128)(2,1)} %pad_maximum_fusion), channel_id=1, source_target_pairs={{0,4},{4,8},{8,12},{12,16},{16,20},{20,24},{24,28},{1,5},{5,9},{9,... | collective-permute-start | bytes 3145736 | tf_op jit(solution)/shard_map/ppermute | solution.py:13
  12.8 369.9 %reduce-scatter.2.cloned.1.call-start = ((), (), s32[]{:S(2)}) async-start(), calls=%async_computation.1 | async-start | bytes 5242880 | tf_op jit(solution)/shard_map/reduce_scatter | solution.py:117
  40.7 52.7 %collective-permute-start.1 = (bf16[2,256,1024]{2,1,0:T(8,128)(2,1)S(1)}, bf16[2,256,1024]{2,1,0:T(8,128)(2,1)S(1)}, u32[]{:S(2)}, u32[]{:S(2)}) collective-permute-start(bf16[2,256,1024]{2,1,0:T(8,128)(2,1)S(1)} %collective-permute-done), channel_id=1, source_target_pairs={{0,4},{4,8},{8,12},{12,16},{16,20},{20,24},{24,28},{1,5},{5,9},{9,... | collective-permute-start | bytes 3145736 | tf_op jit(solution)/shard_map/ppermute | solution.py:13
  93.4 25.9 %collective-permute-start.2 = (bf16[2,256,1024]{2,1,0:T(8,128)(2,1)S(1)}, bf16[2,256,1024]{2,1,0:T(8,128)(2,1)S(1)}, u32[]{:S(2)}, u32[]{:S(2)}) collective-permute-start(bf16[2,256,1024]{2,1,0:T(8,128)(2,1)S(1)} %collective-permute-done.1), channel_id=1, source_target_pairs={{0,4},{4,8},{8,12},{12,16},{16,20},{20,24},{24,28},{1,5},{5,9},{9,... | collective-permute-start | bytes 3145736 | tf_op jit(solution)/shard_map/ppermute | solution.py:13
  120.3 38.8 %collective-permute-start.3 = (bf16[2,256,1024]{2,1,0:T(8,128)(2,1)S(1)}, bf16[2,256,1024]{2,1,0:T(8,128)(2,1)S(1)}, u32[]{:S(2)}, u32[]{:S(2)}) collective-permute-start(bf16[2,256,1024]{2,1,0:T(8,128)(2,1)S(1)} %collective-permute-done.2), channel_id=1, source_target_pairs={{0,4},{4,8},{8,12},{12,16},{16,20},{20,24},{24,28},{1,5},{5,9},{9,... | collective-permute-start | bytes 3145736 | tf_op jit(solution)/shard_map/ppermute | solution.py:13
  160.2 24.4 %collective-permute-start.4 = (bf16[2,256,1024]{2,1,0:T(8,128)(2,1)S(1)}, bf16[2,256,1024]{2,1,0:T(8,128)(2,1)}, u32[]{:S(2)}, u32[]{:S(2)}) collective-permute-start(bf16[2,256,1024]{2,1,0:T(8,128)(2,1)S(1)} %collective-permute-done.3), channel_id=1, source_target_pairs={{0,4},{4,8},{8,12},{12,16},{16,20},{20,24},{24,28},{1,5},{5,9},{9,... | collective-permute-start | bytes 3145736 | tf_op jit(solution)/shard_map/ppermute | solution.py:13
  184.5 46.1 %collective-permute-start.5 = (bf16[2,256,1024]{2,1,0:T(8,128)(2,1)}, bf16[2,256,1024]{2,1,0:T(8,128)(2,1)}, u32[]{:S(2)}, u32[]{:S(2)}) collective-permute-start(bf16[2,256,1024]{2,1,0:T(8,128)(2,1)} %collective-permute-done.4), channel_id=1, source_target_pairs={{0,4},{4,8},{8,12},{12,16},{16,20},{20,24},{24,28},{1,5},{5,9},{9,... | collective-permute-start | bytes 3145736 | tf_op jit(solution)/shard_map/ppermute | solution.py:13
  226.9 5.1 %copy-start.3 = (bf16[2,256,1024]{2,1,0:T(8,128)(2,1)S(1)}, bf16[2,256,1024]{2,1,0:T(8,128)(2,1)}, u32[]{:S(2)}) copy-start(bf16[2,256,1024]{2,1,0:T(8,128)(2,1)} %copy-done.2) | copy-start | bytes 3145732
  228.8 5.1 %copy-start.6 = (bf16[2,256,1024]{2,1,0:T(8,128)(2,1)S(1)}, bf16[2,256,1024]{2,1,0:T(8,128)(2,1)}, u32[]{:S(2)}) copy-start(bf16[2,256,1024]{2,1,0:T(8,128)(2,1)} %copy-done.5) | copy-start | bytes 3145732
  230.7 17.0 %collective-permute-start.6 = (bf16[2,256,1024]{2,1,0:T(8,128)(2,1)}, bf16[2,256,1024]{2,1,0:T(8,128)(2,1)}, u32[]{:S(2)}, u32[]{:S(2)}) collective-permute-start(bf16[2,256,1024]{2,1,0:T(8,128)(2,1)} %collective-permute-done.5), channel_id=1, source_target_pairs={{0,4},{4,8},{8,12},{12,16},{16,20},{20,24},{24,28},{1,5},{5,9},{9,... | collective-permute-start | bytes 3145736 | tf_op jit(solution)/shard_map/ppermute | solution.py:13
  250.8 18.5 %collective-permute-start.7 = (bf16[2,256,1024]{2,1,0:T(8,128)(2,1)}, bf16[2,256,1024]{2,1,0:T(8,128)(2,1)}, u32[]{:S(2)}, u32[]{:S(2)}) collective-permute-start(bf16[2,256,1024]{2,1,0:T(8,128)(2,1)} %collective-permute-done.6), channel_id=1, source_target_pairs={{0,4},{4,8},{8,12},{12,16},{16,20},{20,24},{24,28},{1,5},{5,9},{9,... | collective-permute-start | bytes 3145736 | tf_op jit(solution)/shard_map/ppermute | solution.py:13
  270.7 4.3 %copy-start.7 = (bf16[2,256,1024]{2,1,0:T(8,128)(2,1)S(1)}, bf16[2,256,1024]{2,1,0:T(8,128)(2,1)}, u32[]{:S(2)}) copy-start(bf16[2,256,1024]{2,1,0:T(8,128)(2,1)} %copy-done.5) | copy-start | bytes 3145732
  283.8 3.5 copy-start.24
  295.4 4.0 %copy-start.16 = (bf16[32,8,8,128]{3,2,1,0:T(8,128)(2,1)S(1)}, bf16[32,8,8,128]{3,2,1,0:T(8,128)(2,1)}, u32[]{:S(2)}) copy-start(bf16[32,8,8,128]{3,2,1,0:T(8,128)(2,1)} %copy.33) | copy-start | bytes 1572868
  295.4 4.8 %copy-start.15 = (bf16[32,8,8,128]{3,2,1,0:T(8,128)(2,1)S(1)}, bf16[32,8,8,128]{3,2,1,0:T(8,128)(2,1)}, u32[]{:S(2)}) copy-start(bf16[32,8,8,128]{3,2,1,0:T(8,128)(2,1)} %copy.34) | copy-start | bytes 1572868
  295.4 5.7 %copy-start.13 = (bf16[32,8,8,128]{3,2,1,0:T(8,128)(2,1)S(1)}, bf16[32,8,8,128]{3,2,1,0:T(8,128)(2,1)}, u32[]{:S(2)}) copy-start(bf16[32,8,8,128]{3,2,1,0:T(8,128)(2,1)} %copy.35) | copy-start | bytes 1572868
  295.4 6.5 %copy-start.11 = (bf16[32,8,8,128]{3,2,1,0:T(8,128)(2,1)S(1)}, bf16[32,8,8,128]{3,2,1,0:T(8,128)(2,1)}, u32[]{:S(2)}) copy-start(bf16[32,8,8,128]{3,2,1,0:T(8,128)(2,1)} %copy.36) | copy-start | bytes 1572868
  295.4 7.3 %copy-start.10 = (bf16[32,8,8,128]{3,2,1,0:T(8,128)(2,1)S(1)}, bf16[32,8,8,128]{3,2,1,0:T(8,128)(2,1)}, u32[]{:S(2)}) copy-start(bf16[32,8,8,128]{3,2,1,0:T(8,128)(2,1)} %copy.37) | copy-start | bytes 1572868
  298.2 5.5 %copy-start.9 = (bf16[32,8,8,128]{3,2,1,0:T(8,128)(2,1)S(1)}, bf16[32,8,8,128]{3,2,1,0:T(8,128)(2,1)}, u32[]{:S(2)}) copy-start(bf16[32,8,8,128]{3,2,1,0:T(8,128)(2,1)} %copy.38) | copy-start | bytes 1572868
  316.6 6.2 %slice-start = ((s8[8388608]{0:T(1024)(128)(4,1)}), s8[4194304]{0:T(1024)(128)(4,1)S(1)}, s32[]{:S(2)}) async-start(s8[8388608]{0:T(1024)(128)(4,1)} %bitcast.219), calls=%async_computation.3 | async-start | bytes 8388608
  319.1 3.7 slice-start.1
  (16 other events, 34.0 us)
Sparse Core Ops, SparseCore 0:
  13.0 102.8 all-gather.2
  327.5 55.1 reduce-scatter.1
where the time goes:
time: 395 us; the launch traced here: 392 us
  waiting for transfers between devices  233 us (59%)
  local copies, waits for them, and re-layouts  38.2 us (10%)
  blocking collectives  34.3 us (9%)
  other arithmetic  28.3 us (7%)
  matrix products  28.2 us (7%)
  between operations  19.2 us (5%)
  starting transfers between devices  10.3 us (3%)
    ppermute x8, waiting for transfers between devices, passed_along(): return lax.ppermute(block, axis, route)  177 us
    reduce_scatter x1, waiting for transfers between devices, body(): lax.psum_scatter(partial_out, 'head', scatter_dimension=1, tiled=True)  55.3 us
    unnamed x105, local copies, waits for them, and re-layouts  35 us
    all_gather x1, blocking collectives, prefix(): gathered = jax.tree.map(lambda a: lax.all_gather(a, axis), part)  34.3 us
    ppermute x8, starting transfers between devices, passed_along(): return lax.ppermute(block, axis, route)  10.2 us
    dot_general x8, matrix products, body(): jnp.dot(weights.astype(jnp.bfloat16), value_head, preferred_element_type=...  9.68 us
    add x14, other arithmetic, add_pair(): return (earlier[0] + later[0], earlier[1] + later[1])  8.26 us
  transfers between devices with their start and end apart: 10, of which 8 were waited for; matrix products, arithmetic and copies ran while one was open for 8% of the time, Pallas kernels for 0%

commit v1 on v0

--- a/solution.py
+++ b/solution.py
@@ -1,10 +1,15 @@
+import functools
+
 import jax
 import jax.numpy as jnp
 from jax import lax
+from jax.experimental import pallas as pl
+from jax.experimental.pallas import tpu as pltpu
 from jax.sharding import PartitionSpec as P
 
 HD = 128
 SEG = 2048
+CHUNKS = 2
 
 
 def passed_along(block, axis, distance):
@@ -118,8 +123,266 @@
     return summed.astype(jnp.bfloat16)
 
 
+def exchange_kernel(
+    n_seq, n_head, heads, chunks, beta_ref, q_hbm, k_hbm, v_hbm, w_hbm, out_ref,
+    k_all, v_all, q_all, o_all, q_own, gated_memory, memory, norm_prev, local_own, w_own,
+    to_sibling, from_sibling, kept, to_far, from_far,
+    in_send, in_recv, own_sem, o_send, o_recv, sib_send, sib_recv, far_send, far_recv,
+):
+    me = lax.axis_index("seq")
+    head_rank = lax.axis_index("head")
+    pair = head_rank // 2
+    side = head_rank % 2
+    pairs = n_head // 2
+    sibling = pair * 2 + 1 - side
+    rows = q_own.shape[0]
+    part = rows // chunks
+    out_cols = out_ref.shape[1]
+    offsets = sorted(range(1, n_seq), key=lambda d: abs(d - n_seq // 2))
+
+    def remote(src, dst, send, recv, where):
+        return pltpu.make_async_remote_copy(
+            src_ref=src, dst_ref=dst, send_sem=send, recv_sem=recv,
+            device_id=where, device_id_type=pl.DeviceIdType.MESH,
+        )
+
+    barrier = pltpu.get_barrier_semaphore()
+    for d in range(1, n_seq):
+        pl.semaphore_signal(
+            barrier, inc=1, device_id={"seq": (me + d) % n_seq},
+            device_id_type=pl.DeviceIdType.MESH,
+        )
+    pl.semaphore_signal(
+        barrier, inc=1, device_id={"head": sibling}, device_id_type=pl.DeviceIdType.MESH
+    )
+    for hop in range(1, pairs):
+        pl.semaphore_signal(
+            barrier, inc=1, device_id={"head": ((pair + hop) % pairs) * 2 + side},
+            device_id_type=pl.DeviceIdType.MESH,
+        )
+    pl.semaphore_wait(barrier, n_seq - 1 + 1 + pairs - 1)
+
+    def lanes(index):
+        return pl.ds(pl.multiple_of(index * HD, HD), HD)
+
+    def place(index, start, size):
+        return pl.ds(pl.multiple_of(index * rows + start, part), size)
+
+    def inbound(kind, d):
+        target = (me + d) % n_seq
+        if kind < 2:
+            src, dst, start, size = (k_hbm, k_all, 0, rows) if kind == 0 else (v_hbm, v_all, 0, rows)
+        else:
+            src, dst, start, size = q_hbm, q_all, (kind - 2) * part, part
+        return remote(
+            src.at[pl.ds(start, size), lanes(target)], dst.at[place(me, start, size), :],
+            in_send.at[kind, d], in_recv.at[kind, d], {"seq": target},
+        )
+
+    for kind_group in [(0, 1)] + [(2 + c,) for c in range(chunks)]:
+        for d in offsets:
+            for kind in kind_group:
+                inbound(kind, d).start()
+
+    own_copies = [
+        pltpu.make_async_copy(k_hbm.at[:, lanes(me)], k_all.at[place(me, 0, rows), :], own_sem.at[0]),
+        pltpu.make_async_copy(v_hbm.at[:, lanes(me)], v_all.at[place(me, 0, rows), :], own_sem.at[1]),
+        pltpu.make_async_copy(q_hbm.at[:, lanes(me)], q_all.at[place(me, 0, rows), :], own_sem.at[2]),
+        pltpu.make_async_copy(q_hbm, q_own, own_sem.at[3]),
+        pltpu.make_async_copy(w_hbm, w_own, own_sem.at[4]),
+    ]
+    for copy in own_copies:
+        copy.start()
+
+    memory[...] = jnp.zeros_like(memory)
+    norm_prev[...] = jnp.zeros_like(norm_prev)
+    own_copies[3].wait()
+    for h in range(heads):
+        cols = slice(h * HD, (h + 1) * HD)
+        soft = elu_plus(q_own[:, cols].astype(jnp.float32)).astype(jnp.bfloat16).astype(jnp.float32)
+        numer = jnp.dot(
+            soft, memory[h], precision=lax.Precision.HIGHEST, preferred_element_type=jnp.float32
+        )
+        denom = 1.0 + jnp.sum(soft * norm_prev[h : h + 1, :], axis=1, keepdims=True)
+        gate = jax.nn.sigmoid(jnp.full((1, HD), beta_ref[h], jnp.float32))
+        gated_memory[:, cols] = gate * (numer / denom)
+    for index in range(3):
+        own_copies[index].wait()
+
+    def arrived(kind, source):
+        d = (me - source + n_seq) % n_seq
+
+        @pl.when(source != me)
+        def _():
+            start, size = (0, rows) if kind < 2 else ((kind - 2) * part, part)
+            dst = (k_all, v_all, q_all)[min(kind, 2)].at[place(source, start, size), :]
+            remote(dst, dst, in_send.at[kind, d], in_recv.at[kind, d], {"seq": source}).wait_recv()
+
+    keep_local = 1.0 - jax.nn.sigmoid(jnp.full((1, HD), beta_ref[me], jnp.float32))
+    factor = HD ** (-0.5) * 1.4426950408889634
+    row_at = lax.broadcasted_iota(jnp.int32, (part, part), 0)
+    col_at = lax.broadcasted_iota(jnp.int32, (part, part), 1)
+    contract = (((1,), (1,)), ((), ()))
+
+    def outbound(chunk, block):
+        d = (block - me + n_seq) % n_seq
+        return remote(
+            o_all.at[pl.ds(block * rows + chunk * part, part), :],
+            local_own.at[pl.ds(chunk * part, part), lanes(me)],
+            o_send.at[chunk, d], o_recv.at[chunk, d], {"seq": block},
+        )
+
+    for chunk in range(chunks):
+        for block in range(n_seq):
+            if chunk == 0:
+                arrived(0, block)
+                arrived(1, block)
+            arrived(2 + chunk, block)
+            first = block * rows + chunk * part
+            query = q_all[first : first + part, :]
+            edge = lax.dot_general(
+                query, k_all[first : first + part, :], contract, preferred_element_type=jnp.float32
+            )
+            edge = jnp.where(col_at <= row_at, edge, -jnp.inf)
+            highest = jnp.max(edge, axis=1, keepdims=True)
+            if first:
+                scores = lax.dot_general(
+                    query, k_all[:first, :], contract, preferred_element_type=jnp.float32
+                )
+                highest = jnp.maximum(highest, jnp.max(scores, axis=1, keepdims=True))
+            weights = jnp.exp2((edge - highest) * factor)
+            total = jnp.sum(weights, axis=1, keepdims=True)
+            summed = jnp.dot(
+                weights.astype(jnp.bfloat16), v_all[first : first + part, :],
+                preferred_element_type=jnp.float32,
+            )
+            if first:
+                weights = jnp.exp2((scores - highest) * factor)
+                total = total + jnp.sum(weights, axis=1, keepdims=True)
+                summed = summed + jnp.dot(
+                    weights.astype(jnp.bfloat16), v_all[:first, :],
+                    preferred_element_type=jnp.float32,
+                )
+            result = (keep_local * (summed / total)).astype(jnp.bfloat16)
+            o_all[first : first + part, :] = result
+
+            @pl.when(block != me)
+            def _():
+                outbound(chunk, block).start()
+
+            @pl.when(block == me)
+            def _():
+                local_own[chunk * part : (chunk + 1) * part, lanes(me)] = result
+
+    own_copies[4].wait()
+
+    def sibling_copy(chunk, hop):
+        return remote(
+            to_sibling.at[chunk, hop], from_sibling.at[chunk, hop],
+            sib_send.at[chunk, hop], sib_recv.at[chunk, hop], {"head": sibling},
+        )
+
+    def far_copy(chunk, hop):
+        return remote(
+            to_far.at[chunk, hop - 1], from_far.at[chunk, hop - 1],
+            far_send.at[chunk, hop - 1], far_recv.at[chunk, hop - 1],
+            {"head": ((pair + hop) % pairs) * 2 + side},
+        )
+
+    hops = list(range(1, pairs)) + [0]
+    for chunk in range(chunks):
+        span = slice(chunk * part, (chunk + 1) * part)
+        for d in range(1, n_seq):
+            source = (me - d + n_seq) % n_seq
+            dst = local_own.at[pl.ds(chunk * part, part), lanes(source)]
+            remote(dst, dst, o_send.at[chunk, d], o_recv.at[chunk, d], {"seq": source}).wait_recv()
+        attended = (local_own[span, :].astype(jnp.float32) + gated_memory[span, :]).astype(jnp.bfloat16)
+
+        def share(index):
+            cols = pl.ds(pl.multiple_of(index * out_cols, out_cols), out_cols)
+            return jnp.dot(attended, w_own[:, cols], preferred_element_type=jnp.float32)
+
+        for hop in hops:
+            base = ((pair + hop) % pairs) * 2
+            to_sibling[chunk, hop] = share(base + 1 - side).astype(jnp.bfloat16)
+            sibling_copy(chunk, hop).start()
+            kept[chunk, hop] = share(base + side)
+            if hop:
+                sibling_copy(chunk, hop).wait_recv()
+                to_far[chunk, hop - 1] = (
+                    kept[chunk, hop] + from_sibling[chunk, hop].astype(jnp.float32)
+                ).astype(jnp.bfloat16)
+                far_copy(chunk, hop).start()
+
+    for chunk in range(chunks):
+        span = slice(chunk * part, (chunk + 1) * part)
+        sibling_copy(chunk, 0).wait_recv()
+        result = kept[chunk, 0] + from_sibling[chunk, 0].astype(jnp.float32)
+        for hop in range(1, pairs):
+            far_copy(chunk, hop).wait_recv()
+            result = result + from_far[chunk, hop - 1].astype(jnp.float32)
+        out_ref[span, :] = result.astype(out_ref.dtype)
+
+    for kind in range(2 + chunks):
+        for d in offsets:
+            inbound(kind, d).wait_send()
+    for chunk in range(chunks):
+        for block in range(n_seq):
+            @pl.when(block != me)
+            def _():
+                outbound(chunk, block).wait_send()
+        for hop in range(pairs):
+            sibling_copy(chunk, hop).wait_send()
+            if hop:
+                far_copy(chunk, hop).wait_send()
+
+
+def one_segment_body(n_seq, n_head, queries, keys, values, beta, w_out):
+    rows, width = queries.shape
+    heads = width // HD
+    tokens = rows * n_seq
+    out_cols = w_out.shape[1] // n_head
+    pairs = n_head // 2
+    chunks = CHUNKS
+    part = rows // chunks
+    vmem, dma = pltpu.VMEM, pltpu.SemaphoreType.DMA
+    half, full = jnp.bfloat16, jnp.float32
+    anywhere = pl.BlockSpec(memory_space=pl.ANY)
+    return pl.pallas_call(
+        functools.partial(exchange_kernel, n_seq, n_head, heads, chunks),
+        out_shape=jax.ShapeDtypeStruct((rows, out_cols), half),
+        in_specs=[pl.BlockSpec(memory_space=pltpu.SMEM)] + [anywhere] * 4,
+        out_specs=pl.BlockSpec(memory_space=pltpu.VMEM),
+        scratch_shapes=[
+            vmem((tokens, HD), half), vmem((tokens, HD), half), vmem((tokens, HD), half),
+            vmem((tokens, HD), half), vmem((rows, width), half), vmem((rows, width), full),
+            vmem((heads, HD, HD), full), vmem((heads, HD), full), vmem((rows, width), half),
+            vmem(w_out.shape, half),
+            vmem((chunks, pairs, part, out_cols), half), vmem((chunks, pairs, part, out_cols), half),
+            vmem((chunks, pairs, part, out_cols), full),
+            vmem((chunks, max(pairs - 1, 1), part, out_cols), half),
+            vmem((chunks, max(pairs - 1, 1), part, out_cols), half),
+            dma((2 + chunks, n_seq)), dma((2 + chunks, n_seq)), dma((5,)),
+            dma((chunks, n_seq)), dma((chunks, n_seq)),
+            dma((chunks, pairs)), dma((chunks, pairs)),
+            dma((chunks, max(pairs - 1, 1))), dma((chunks, max(pairs - 1, 1))),
+        ],
+        compiler_params=pltpu.CompilerParams(
+            collective_id=0, has_side_effects=True, vmem_limit_bytes=50 * 1024 * 1024
+        ),
+    )(beta, queries, keys, values, w_out)
+
+
 def solution(mesh):
     placed = (P("seq", "head"), P("seq", "head"), P("seq", "head"), P("head"), P("head", None))
+    n_seq, n_head = mesh.shape["seq"], mesh.shape["head"]
+
+    def chosen(queries, keys, values, beta, w_out):
+        rows, width = queries.shape
+        if rows * n_seq == SEG and width == HD * n_seq and n_head % 2 == 0:
+            return one_segment_body(n_seq, n_head, queries, keys, values, beta, w_out)
+        return body(queries, keys, values, beta, w_out)
+
     return jax.shard_map(
-        body, mesh=mesh, in_specs=placed, out_specs=P("seq", "head"), check_vma=False
-    )
+        chosen, mesh=mesh, in_specs=placed, out_specs=P("seq", "head"), check_vma=False
+    )

time: 395 us -> 69.5 us (0.18)
  waiting for transfers between devices: 233 us -> 0 us
  Pallas kernels: 0 us -> 64.5 us
  blocking collectives: 34.3 us -> 0 us
  local copies, waits for them, and re-layouts: 38.2 us -> 4.57 us
  other arithmetic: 28.3 us -> 0 us
  matrix products: 28.2 us -> 0 us
  between operations: 19.2 us -> 0.01 us
  starting transfers between devices: 10.3 us -> 0 us
    ppermute x8 -> x0, waiting for transfers between devices: 177 us -> none  [passed_along(): return lax.ppermute(block, axis, route)]
    pallas_call x0 -> x1, Pallas kernels: none -> 64.5 us  [one_segment_body(): pl.pallas_call(functools.partial(exchange_kernel, n_seq, n_head, heads, c...]
    reduce_scatter x1 -> x0, waiting for transfers between devices: 55.3 us -> none  [body(): lax.psum_scatter(partial_out, 'head', scatter_dimension=1, tiled=True)]
    all_gather x1 -> x0, blocking collectives: 34.3 us -> none  [prefix(): gathered = jax.tree.map(lambda a: lax.all_gather(a, axis), part)]
    unnamed x105 -> x9, local copies, waits for them, and re-layouts: 35 us -> 4.57 us
    dot_general x21 -> x0, matrix products: 28.2 us -> none  [the longest x8 9.68 us: body(): jnp.dot(weights.astype(jnp.bfloat16), value_head, preferred_element_type=...]
    ppermute x8 -> x0, starting transfers between devices: 10.2 us -> none  [passed_along(): return lax.ppermute(block, axis, route)]
    add x15 -> x0, other arithmetic: 8.27 us -> none  [the longest x14 8.26 us: add_pair(): return (earlier[0] + later[0], earlier[1] + later[1])]
  transfers between devices with their start and end apart: 10 -> 0, of which waited for: 8 -> 0; matrix products, arithmetic and copies ran while one was open for 8% -> 0% of each run, Pallas kernels for 0% -> 0%
where the time goes in v1:
time: 69.5 us; the launch traced here: 69.1 us
  Pallas kernels  64.5 us (93%)
  local copies, waits for them, and re-layouts  4.57 us (7%)
    pallas_call x1, Pallas kernels, one_segment_body(): pl.pallas_call(functools.partial(exchange_kernel, n_seq, n_head, heads, c...  64.5 us
    unnamed x9, local copies, waits for them, and re-layouts  4.57 us

profile of v1, /device:TPU:29, one launch (start us, length us, event | category | flops | bytes accessed | tf_op | source)
XLA Modules:
  0.0 69.1 jit_solution(4056556523705425130)
XLA Ops:
  0.0 0.0 copy-start
  0.0 1.0 %copy-done = bf16[256,1024]{1,0:T(8,128)(2,1)S(1)} copy-done((bf16[256,1024]{1,0:T(8,128)(2,1)S(1)}, bf16[256,1024]{1,0:T(8,128)(2,1)}, u32[]{:S(2)}) %copy-start) | copy-done | bytes 524312
  1.0 0.0 copy-start.1
  1.0 1.0 %copy-done.1 = bf16[256,1024]{1,0:T(8,128)(2,1)S(1)} copy-done((bf16[256,1024]{1,0:T(8,128)(2,1)S(1)}, bf16[256,1024]{1,0:T(8,128)(2,1)}, u32[]{:S(2)}) %copy-start.1) | copy-done | bytes 524312
  2.1 0.0 copy-start.2
  2.1 1.0 %copy-done.2 = bf16[256,1024]{1,0:T(8,128)(2,1)S(1)} copy-done((bf16[256,1024]{1,0:T(8,128)(2,1)S(1)}, bf16[256,1024]{1,0:T(8,128)(2,1)}, u32[]{:S(2)}) %copy-start.2) | copy-done | bytes 524312
  3.1 0.0 copy-start.3
  3.1 0.7 copy-done.3
  3.8 64.5 %shard_map.55 = bf16[256,1024]{1,0:T(8,128)(2,1)S(1)} custom-call(f32[8]{0:T(128)S(1)} %copy-done.3, bf16[256,1024]{1,0:T(8,128)(2,1)S(1)} %copy-done, bf16[256,1024]{1,0:T(8,128)(2,1)S(1)} %copy-done.1, bf16[256,1024]{1,0:T(8,128)(2,1)S(1)} %copy-done.2, bf16[1024,4096]{1,0:T(8,128)(2,1)} %w_hbm.1), custom_call_target="tpu_custom_call" | custom-call | tf_op jit(solution)/shard_map/pallas_call | solution.py:351
  68.3 0.8 %copy.7 = bf16[256,1024]{1,0:T(8,128)(2,1)} copy(bf16[256,1024]{1,0:T(8,128)(2,1)S(1)} %shard_map.55) | data formatting | bytes 1048576
Async XLA Ops:
  0.0 1.0 %copy-start = (bf16[256,1024]{1,0:T(8,128)(2,1)S(1)}, bf16[256,1024]{1,0:T(8,128)(2,1)}, u32[]{:S(2)}) copy-start(bf16[256,1024]{1,0:T(8,128)(2,1)} %q_hbm.1) | copy-start | bytes 1572868
  1.0 1.0 %copy-start.1 = (bf16[256,1024]{1,0:T(8,128)(2,1)S(1)}, bf16[256,1024]{1,0:T(8,128)(2,1)}, u32[]{:S(2)}) copy-start(bf16[256,1024]{1,0:T(8,128)(2,1)} %k_hbm.1) | copy-start | bytes 1572868
  2.1 1.0 %copy-start.2 = (bf16[256,1024]{1,0:T(8,128)(2,1)S(1)}, bf16[256,1024]{1,0:T(8,128)(2,1)}, u32[]{:S(2)}) copy-start(bf16[256,1024]{1,0:T(8,128)(2,1)} %v_hbm.1) | copy-start | bytes 1572868
  3.1 0.7 copy-start.3

commit v2 on v1

--- a/solution.py
+++ b/solution.py
@@ -10,6 +10,7 @@
 HD = 128
 SEG = 2048
 CHUNKS = 2
+QUARTERS = 4
 
 
 def passed_along(block, axis, distance):
@@ -125,9 +126,11 @@
 
 def exchange_kernel(
     n_seq, n_head, heads, chunks, beta_ref, q_hbm, k_hbm, v_hbm, w_hbm, out_ref,
-    k_all, v_all, q_all, o_all, q_own, gated_memory, memory, norm_prev, local_own, w_own,
+    k_all, v_all, q_all, o_all, sums_all, q_own, gated_memory, memory, norm_prev,
+    parts, sums, attended_own, w_own,
     to_sibling, from_sibling, kept, to_far, from_far,
-    in_send, in_recv, own_sem, o_send, o_recv, sib_send, sib_recv, far_send, far_recv,
+    in_send, in_recv, own_sem, o_send, o_recv, sums_send, sums_recv,
+    sib_send, sib_recv, far_send, far_recv,
 ):
     me = lax.axis_index("seq")
     head_rank = lax.axis_index("head")
@@ -138,7 +141,12 @@
     rows = q_own.shape[0]
     part = rows // chunks
     out_cols = out_ref.shape[1]
-    offsets = sorted(range(1, n_seq), key=lambda d: abs(d - n_seq // 2))
+    group = n_seq // QUARTERS
+    quarter = me // group
+    mine = me % group
+    many = heads // group
+    wide = many * HD
+    held = group * rows
 
     def remote(src, dst, send, recv, where):
         return pltpu.make_async_remote_copy(
@@ -165,29 +173,68 @@
     def lanes(index):
         return pl.ds(pl.multiple_of(index * HD, HD), HD)
 
-    def place(index, start, size):
-        return pl.ds(pl.multiple_of(index * rows + start, part), size)
-
-    def inbound(kind, d):
-        target = (me + d) % n_seq
-        if kind < 2:
-            src, dst, start, size = (k_hbm, k_all, 0, rows) if kind == 0 else (v_hbm, v_all, 0, rows)
-        else:
-            src, dst, start, size = q_hbm, q_all, (kind - 2) * part, part
+    sources = (k_hbm, v_hbm, q_hbm, k_hbm, v_hbm, q_hbm, q_hbm)
+    landing = (k_all, v_all, q_all, k_all, v_all, q_all, q_all)
+    base_row = (held, held, 0, 0, 0, held, 2 * held)
+
+    def moved(kind, channel, head, there, to_quarter):
         return remote(
-            src.at[pl.ds(start, size), lanes(target)], dst.at[place(me, start, size), :],
-            in_send.at[kind, d], in_recv.at[kind, d], {"seq": target},
-        )
-
-    for kind_group in [(0, 1)] + [(2 + c,) for c in range(chunks)]:
-        for d in offsets:
-            for kind in kind_group:
-                inbound(kind, d).start()
-
+            sources[kind].at[:, lanes(there * many + head)],
+            landing[kind].at[
+                pl.ds(pl.multiple_of(base_row[kind] + mine * rows, rows), rows), lanes(head)
+            ],
+            in_send.at[channel, head, there], in_recv.at[kind, head, mine],
+            {"seq": to_quarter * group + there},
+        )
+
+    def landed(kind, head, source):
+        dst = landing[kind].at[pl.ds(base_row[kind] + source * rows, rows), lanes(head)]
+        return remote(
+            dst, dst, in_send.at[kind, head, source], in_recv.at[kind, head, source],
+            {"seq": (me + 1) % n_seq},
+        )
+
+    def plan(role):
+        sends = []
+        if role == 0:
+            sends += [(3, 3, 1), (4, 4, 1)]
+        if role == 2:
+            sends += [(5, 5, 1)]
+        if role == 3:
+            sends += [(6, 5, 1), (6, 6, 2)]
+        return sends
+
+    def in_role(role, action):
+        pl.when(quarter == role)(action)
+
+    def each_send(role, action):
+        def one(head, carry):
+            for kind, channel, to_quarter in plan(role):
+                for there in range(group):
+                    action(moved(kind, channel, head, there, to_quarter))
+            for there in range(group):
+                @pl.when(there != mine)
+                def _():
+                    for kind in range(3):
+                        action(moved(kind, kind, head, there, role))
+            return carry
+
+        lax.fori_loop(0, many, one, 0)
+
+    for role in range(QUARTERS):
+        in_role(role, functools.partial(each_send, role, lambda copy: copy.start()))
+
+    block = pl.ds(pl.multiple_of(mine * wide, wide), wide)
     own_copies = [
-        pltpu.make_async_copy(k_hbm.at[:, lanes(me)], k_all.at[place(me, 0, rows), :], own_sem.at[0]),
-        pltpu.make_async_copy(v_hbm.at[:, lanes(me)], v_all.at[place(me, 0, rows), :], own_sem.at[1]),
-        pltpu.make_async_copy(q_hbm.at[:, lanes(me)], q_all.at[place(me, 0, rows), :], own_sem.at[2]),
+        pltpu.make_async_copy(
+            source.at[:, block],
+            place.at[pl.ds(pl.multiple_of(start + mine * rows, rows), rows), :], own_sem.at[i],
+        )
+        for i, (source, place, start) in enumerate(
+            ((k_hbm, k_all, held), (v_hbm, v_all, held), (q_hbm, q_all, 0))
+        )
+    ]
+    own_copies += [
         pltpu.make_async_copy(q_hbm, q_own, own_sem.at[3]),
         pltpu.make_async_copy(w_hbm, w_own, own_sem.at[4]),
     ]
@@ -197,6 +244,10 @@
     memory[...] = jnp.zeros_like(memory)
     norm_prev[...] = jnp.zeros_like(norm_prev)
     own_copies[3].wait()
+
+    def gate_of(h):
+        return jax.nn.sigmoid(jnp.full((1, HD), beta_ref[h], jnp.float32))
+
     for h in range(heads):
         cols = slice(h * HD, (h + 1) * HD)
         soft = elu_plus(q_own[:, cols].astype(jnp.float32)).astype(jnp.bfloat16).astype(jnp.float32)
@@ -204,75 +255,158 @@
             soft, memory[h], precision=lax.Precision.HIGHEST, preferred_element_type=jnp.float32
         )
         denom = 1.0 + jnp.sum(soft * norm_prev[h : h + 1, :], axis=1, keepdims=True)
-        gate = jax.nn.sigmoid(jnp.full((1, HD), beta_ref[h], jnp.float32))
-        gated_memory[:, cols] = gate * (numer / denom)
+        gated_memory[:, cols] = gate_of(h) * (numer / denom)
+
+    for slot in (1, 2):
+        @pl.when(quarter <= slot)
+        def _():
+            parts[slot] = jnp.zeros(parts.shape[1:], parts.dtype)
+            sums[slot] = jnp.full(sums.shape[1:], -1e30, sums.dtype)
+
     for index in range(3):
         own_copies[index].wait()
 
-    def arrived(kind, source):
-        d = (me - source + n_seq) % n_seq
-
-        @pl.when(source != me)
-        def _():
-            start, size = (0, rows) if kind < 2 else ((kind - 2) * part, part)
-            dst = (k_all, v_all, q_all)[min(kind, 2)].at[place(source, start, size), :]
-            remote(dst, dst, in_send.at[kind, d], in_recv.at[kind, d], {"seq": source}).wait_recv()
-
-    keep_local = 1.0 - jax.nn.sigmoid(jnp.full((1, HD), beta_ref[me], jnp.float32))
     factor = HD ** (-0.5) * 1.4426950408889634
-    row_at = lax.broadcasted_iota(jnp.int32, (part, part), 0)
-    col_at = lax.broadcasted_iota(jnp.int32, (part, part), 1)
     contract = (((1,), (1,)), ((), ()))
 
-    def outbound(chunk, block):
-        d = (block - me + n_seq) % n_seq
-        return remote(
-            o_all.at[pl.ds(block * rows + chunk * part, part), :],
-            local_own.at[pl.ds(chunk * part, part), lanes(me)],
-            o_send.at[chunk, d], o_recv.at[chunk, d], {"seq": block},
-        )
-
-    for chunk in range(chunks):
-        for block in range(n_seq):
-            if chunk == 0:
-                arrived(0, block)
-                arrived(1, block)
-            arrived(2 + chunk, block)
-            first = block * rows + chunk * part
-            query = q_all[first : first + part, :]
+    def tile(query, cols, low, high, edge_size):
+        pieces = []
+        split = high - edge_size
+        if edge_size:
+            size = query.shape[0]
             edge = lax.dot_general(
-                query, k_all[first : first + part, :], contract, preferred_element_type=jnp.float32
+                query, k_all[split:high, cols], contract, preferred_element_type=jnp.float32
             )
-            edge = jnp.where(col_at <= row_at, edge, -jnp.inf)
-            highest = jnp.max(edge, axis=1, keepdims=True)
-            if first:
-                scores = lax.dot_general(
-                    query, k_all[:first, :], contract, preferred_element_type=jnp.float32
-                )
-                highest = jnp.maximum(highest, jnp.max(scores, axis=1, keepdims=True))
-            weights = jnp.exp2((edge - highest) * factor)
-            total = jnp.sum(weights, axis=1, keepdims=True)
-            summed = jnp.dot(
-                weights.astype(jnp.bfloat16), v_all[first : first + part, :],
+            row_at = lax.broadcasted_iota(jnp.int32, (size, edge_size), 0)
+            col_at = lax.broadcasted_iota(jnp.int32, (size, edge_size), 1)
+            pieces.append((jnp.where(col_at <= row_at, edge, -jnp.inf), split, high))
+        if split > low:
+            scores = lax.dot_general(
+                query, k_all[low:split, cols], contract, preferred_element_type=jnp.float32
+            )
+            pieces.append((scores, low, split))
+        highest = functools.reduce(
+            jnp.maximum, [jnp.max(p, axis=1, keepdims=True) for p, _, _ in pieces]
+        )
+        total, summed = 0.0, 0.0
+        for scores, first, last in pieces:
+            weights = jnp.exp2((scores - highest) * factor)
+            total = total + jnp.sum(weights, axis=1, keepdims=True)
+            summed = summed + jnp.dot(
+                weights.astype(jnp.bfloat16), v_all[first:last, cols],
                 preferred_element_type=jnp.float32,
             )
-            if first:
-                weights = jnp.exp2((scores - highest) * factor)
-                total = total + jnp.sum(weights, axis=1, keepdims=True)
-                summed = summed + jnp.dot(
-                    weights.astype(jnp.bfloat16), v_all[:first, :],
-                    preferred_element_type=jnp.float32,
+        level = highest * factor + jnp.log(total) * 1.4426950408889634
+        return (summed / total).astype(jnp.bfloat16), level
+
+    def returned(q_slot, head, there, to_quarter, slot):
+        where = {"seq": to_quarter * group + there}
+        index = mine * many + head
+        return (
+            remote(
+                o_all.at[q_slot, there, :, lanes(head)], parts.at[slot, :, lanes(index)],
+                o_send.at[q_slot, head, there], o_recv.at[slot, index], where,
+            ),
+            remote(
+                sums_all.at[q_slot, there, head], sums.at[slot, index],
+                sums_send.at[q_slot, head, there], sums_recv.at[slot, index], where,
+            ),
+        )
+
+    def run_block(q_slot, head, there, low, causal):
+        cols = lanes(head)
+        for start in range(0, rows, part):
+            at = there * rows + start
+            query = q_all[q_slot * held + at : q_slot * held + at + part, cols]
+            high = held + at + part if causal else 2 * held
+            out, level = tile(query, cols, low, high, part if causal else 0)
+            o_all[q_slot, there, start : start + part, cols] = out
+            turned = jnp.transpose(jnp.broadcast_to(level, (part, HD)))
+            sums_all[q_slot, there, head, :, start : start + part] = turned[:1, :]
+
+    def wait_pair(head, kinds, own):
+        for source in range(group):
+            def go():
+                for kind in kinds:
+                    landed(kind, head, source).wait_recv()
+            if own:
+                pl.when(source != mine)(go)
+            else:
+                go()
+
+    away = {1: [(1, 5, 0, 2, 1), (2, 6, 0, 3, 1)], 2: [(2, 6, held, 3, 2)]}
+
+    def attend(role):
+        low = 0 if role == 1 else held
+
+        def one(head, carry):
+            wait_pair(head, (0, 1, 2), True)
+            if role == 1:
+                wait_pair(head, (3, 4), False)
+            for q_slot, kind, first, to_quarter, slot in away.get(role, []):
+                for there in range(group):
+                    landed(kind, head, there).wait_recv()
+                    run_block(q_slot, head, there, first, False)
+                    for copy in returned(q_slot, head, there, to_quarter, slot):
+                        copy.start()
+            for there in range(group):
+                run_block(0, head, there, low, True)
+
+                @pl.when(there != mine)
+                def _():
+                    for copy in returned(0, head, there, role, 0):
+                        copy.start()
+
+                @pl.when(there == mine)
+                def _():
+                    index = mine * many + head
+                    parts[0, :, lanes(index)] = o_all[0, there, :, lanes(head)]
+                    sums[0, index] = sums_all[0, there, head]
+            return carry
+
+        lax.fori_loop(0, many, one, 0)
+
+    for role in range(QUARTERS):
+        in_role(role, functools.partial(attend, role))
+
+    def wait_part(slot, index):
+        dst, level = parts.at[slot, :, lanes(index)], sums.at[slot, index]
+        where = {"seq": (me + 1) % n_seq}
+        remote(dst, dst, o_send.at[0, 0, 0], o_recv.at[slot, index], where).wait_recv()
+        remote(level, level, sums_send.at[0, 0, 0], sums_recv.at[slot, index], where).wait_recv()
+
+    def merge(head, carry):
+        for there in range(group):
+            index = there * many + head
+
+            @pl.when(there != mine)
+            def _():
+                wait_part(0, index)
+
+            for slot in (1, 2):
+                @pl.when(quarter > slot)
+                def _():
+                    wait_part(slot, index)
+
+            for start in range(0, rows, part):
+                span = slice(start, start + part)
+                levels = [
+                    jnp.transpose(jnp.broadcast_to(sums[slot, index, :, span], (HD, part)))
+                    for slot in range(3)
+                ]
+                top = functools.reduce(jnp.maximum, levels)
+                shares = [jnp.exp2(level - top) for level in levels]
+                mixed = sum(
+                    share * parts[slot, span, lanes(index)].astype(jnp.float32)
+                    for slot, share in enumerate(shares)
                 )
-            result = (keep_local * (summed / total)).astype(jnp.bfloat16)
-            o_all[first : first + part, :] = result
-
-            @pl.when(block != me)
-            def _():
-                outbound(chunk, block).start()
-
-            @pl.when(block == me)
-            def _():
-                local_own[chunk * part : (chunk + 1) * part, lanes(me)] = result
+                local = mixed / sum(shares)
+                attended_own[span, lanes(index)] = (
+                    gated_memory[span, lanes(index)] + (1.0 - gate_of(index)) * local
+                ).astype(jnp.bfloat16)
+        return carry
+
+    lax.fori_loop(0, many, merge, 0)
 
     own_copies[4].wait()
 
@@ -292,11 +426,7 @@
     hops = list(range(1, pairs)) + [0]
     for chunk in range(chunks):
         span = slice(chunk * part, (chunk + 1) * part)
-        for d in range(1, n_seq):
-            source = (me - d + n_seq) % n_seq
-            dst = local_own.at[pl.ds(chunk * part, part), lanes(source)]
-            remote(dst, dst, o_send.at[chunk, d], o_recv.at[chunk, d], {"seq": source}).wait_recv()
-        attended = (local_own[span, :].astype(jnp.float32) + gated_memory[span, :]).astype(jnp.bfloat16)
+        attended = attended_own[span, :]
 
         def share(index):
             cols = pl.ds(pl.multiple_of(index * out_cols, out_cols), out_cols)
@@ -323,14 +453,26 @@
             result = result + from_far[chunk, hop - 1].astype(jnp.float32)
         out_ref[span, :] = result.astype(out_ref.dtype)
 
-    for kind in range(2 + chunks):
-        for d in offsets:
-            inbound(kind, d).wait_send()
+    for role in range(QUARTERS):
+        def finish(role=role):
+            each_send(role, lambda copy: copy.wait_send())
+
+            def one(head, carry):
+                for q_slot, _, _, to_quarter, slot in away.get(role, []):
+                    for there in range(group):
+                        for copy in returned(q_slot, head, there, to_quarter, slot):
+                            copy.wait_send()
+                for there in range(group):
+                    @pl.when(there != mine)
+                    def _():
+                        for copy in returned(0, head, there, role, 0):
+                            copy.wait_send()
+                return carry
+
+            lax.fori_loop(0, many, one, 0)
+
+        in_role(role, finish)
     for chunk in range(chunks):
-        for block in range(n_seq):
-            @pl.when(block != me)
-            def _():
-                outbound(chunk, block).wait_send()
         for hop in range(pairs):
             sibling_copy(chunk, hop).wait_send()
             if hop:
@@ -340,7 +482,9 @@
 def one_segment_body(n_seq, n_head, queries, keys, values, beta, w_out):
     rows, width = queries.shape
     heads = width // HD
-    tokens = rows * n_seq
+    group = n_seq // QUARTERS
+    many = heads // group
+    wide, held = many * HD, group * rows
     out_cols = w_out.shape[1] // n_head
     pairs = n_head // 2
     chunks = CHUNKS
@@ -354,16 +498,18 @@
         in_specs=[pl.BlockSpec(memory_space=pltpu.SMEM)] + [anywhere] * 4,
         out_specs=pl.BlockSpec(memory_space=pltpu.VMEM),
         scratch_shapes=[
-            vmem((tokens, HD), half), vmem((tokens, HD), half), vmem((tokens, HD), half),
-            vmem((tokens, HD), half), vmem((rows, width), half), vmem((rows, width), full),
-            vmem((heads, HD, HD), full), vmem((heads, HD), full), vmem((rows, width), half),
-            vmem(w_out.shape, half),
+            vmem((2 * held, wide), half), vmem((2 * held, wide), half), vmem((3 * held, wide), half),
+            vmem((3, group, rows, wide), half), vmem((3, group, many, 1, rows), full),
+            vmem((rows, width), half), vmem((rows, width), full),
+            vmem((heads, HD, HD), full), vmem((heads, HD), full),
+            vmem((3, rows, width), half), vmem((3, heads, 1, rows), full),
+            vmem((rows, width), half), vmem(w_out.shape, half),
             vmem((chunks, pairs, part, out_cols), half), vmem((chunks, pairs, part, out_cols), half),
             vmem((chunks, pairs, part, out_cols), full),
             vmem((chunks, max(pairs - 1, 1), part, out_cols), half),
             vmem((chunks, max(pairs - 1, 1), part, out_cols), half),
-            dma((2 + chunks, n_seq)), dma((2 + chunks, n_seq)), dma((5,)),
-            dma((chunks, n_seq)), dma((chunks, n_seq)),
+            dma((7, many, group)), dma((7, many, group)), dma((5,)),
+            dma((3, many, group)), dma((3, heads)), dma((3, many, group)), dma((3, heads)),
             dma((chunks, pairs)), dma((chunks, pairs)),
             dma((chunks, max(pairs - 1, 1))), dma((chunks, max(pairs - 1, 1))),
         ],
@@ -379,7 +525,8 @@
 
     def chosen(queries, keys, values, beta, w_out):
         rows, width = queries.shape
-        if rows * n_seq == SEG and width == HD * n_seq and n_head % 2 == 0:
+        fits = rows == CHUNKS * HD and n_head % 2 == 0 and width // HD * QUARTERS % n_seq == 0
+        if rows * n_seq == SEG and n_seq % QUARTERS == 0 and fits:
             return one_segment_body(n_seq, n_head, queries, keys, values, beta, w_out)
         return body(queries, keys, values, beta, w_out)
 

time: 69.5 us -> 79.6 us (1.15)
  Pallas kernels: 64.5 us -> 74.8 us
    pallas_call x1, Pallas kernels: 64.5 us -> 74.8 us  [one_segment_body(): pl.pallas_call(functools.partial(exchange_kernel, n_seq, n_head, heads, c...]
where the time goes in v2:
time: 79.6 us; the launch traced here: 79.3 us
  Pallas kernels  74.8 us (94%)
  local copies, waits for them, and re-layouts  4.57 us (6%)
    pallas_call x1, Pallas kernels, one_segment_body(): pl.pallas_call(functools.partial(exchange_kernel, n_seq, n_head, heads, c...  74.8 us
    unnamed x9, local copies, waits for them, and re-layouts  4.57 us

profile of v2, /device:TPU:29, one launch (start us, length us, event | category | flops | bytes accessed | tf_op | source)
XLA Modules:
  0.0 79.3 jit_solution(5590146614379852939)
XLA Ops:
  0.0 0.0 copy-start
  0.0 1.0 %copy-done = bf16[256,1024]{1,0:T(8,128)(2,1)S(1)} copy-done((bf16[256,1024]{1,0:T(8,128)(2,1)S(1)}, bf16[256,1024]{1,0:T(8,128)(2,1)}, u32[]{:S(2)}) %copy-start) | copy-done | bytes 524312
  1.0 0.0 copy-start.1
  1.0 1.0 %copy-done.1 = bf16[256,1024]{1,0:T(8,128)(2,1)S(1)} copy-done((bf16[256,1024]{1,0:T(8,128)(2,1)S(1)}, bf16[256,1024]{1,0:T(8,128)(2,1)}, u32[]{:S(2)}) %copy-start.1) | copy-done | bytes 524312
  2.1 0.0 copy-start.2
  2.1 1.0 %copy-done.2 = bf16[256,1024]{1,0:T(8,128)(2,1)S(1)} copy-done((bf16[256,1024]{1,0:T(8,128)(2,1)S(1)}, bf16[256,1024]{1,0:T(8,128)(2,1)}, u32[]{:S(2)}) %copy-start.2) | copy-done | bytes 524312
  3.1 0.0 copy-start.3
  3.1 0.7 copy-done.3
  3.8 74.8 %shard_map.55 = bf16[256,1024]{1,0:T(8,128)(2,1)S(1)} custom-call(f32[8]{0:T(128)S(1)} %copy-done.3, bf16[256,1024]{1,0:T(8,128)(2,1)S(1)} %copy-done, bf16[256,1024]{1,0:T(8,128)(2,1)S(1)} %copy-done.1, bf16[256,1024]{1,0:T(8,128)(2,1)S(1)} %copy-done.2, bf16[1024,4096]{1,0:T(8,128)(2,1)} %w_hbm.1), custom_call_target="tpu_custom_call" | custom-call | tf_op jit(solution)/shard_map/pallas_call | solution.py:495
  78.5 0.8 %copy.7 = bf16[256,1024]{1,0:T(8,128)(2,1)} copy(bf16[256,1024]{1,0:T(8,128)(2,1)S(1)} %shard_map.55) | data formatting | bytes 1048576
Async XLA Ops:
  0.0 1.0 %copy-start = (bf16[256,1024]{1,0:T(8,128)(2,1)S(1)}, bf16[256,1024]{1,0:T(8,128)(2,1)}, u32[]{:S(2)}) copy-start(bf16[256,1024]{1,0:T(8,128)(2,1)} %q_hbm.1) | copy-start | bytes 1572868
  1.0 1.0 %copy-start.1 = (bf16[256,1024]{1,0:T(8,128)(2,1)S(1)}, bf16[256,1024]{1,0:T(8,128)(2,1)}, u32[]{:S(2)}) copy-start(bf16[256,1024]{1,0:T(8,128)(2,1)} %k_hbm.1) | copy-start | bytes 1572868
  2.1 1.0 %copy-start.2 = (bf16[256,1024]{1,0:T(8,128)(2,1)S(1)}, bf16[256,1024]{1,0:T(8,128)(2,1)}, u32[]{:S(2)}) copy-start(bf16[256,1024]{1,0:T(8,128)(2,1)} %v_hbm.1) | copy-start | bytes 1572868
  3.1 0.7 copy-start.3
